TPU v7x, 32 devices: a whole 2x2x4 slice. The times are simulated.
32 devices in a mesh: dp: 8 (over z, x), expert: 4 (over y, core).
Axes of the slice: x: 2, y: 2, z: 4, core: 2. Of those that a mesh axis runs over, the one named last changes fastest.
Arguments:
- tokens: bfloat16 [2048, 2048], P('dp'), may hold values from -6 to 6
- routes: int32 [2048, 6], P('dp'), may hold values from 0 to 63, all different within a row; in each aligned block of 256 rows (0 to 255, 256 to 511, ...) at most 32 rows name the same one
- gates: float32 [2048, 6], P('dp'), may hold values from 0.1 to 1
- w_gate: bfloat16 [64, 2048, 1408], P('dp', None, 'expert'), may hold values from -0.125 to 0.125
- w_up: bfloat16 [64, 2048, 1408], P('dp', None, 'expert'), may hold values from -0.125 to 0.125
- w_down: bfloat16 [64, 1408, 2048], P('dp', 'expert'), may hold values from -0.21875 to 0.21875
- s_gate: bfloat16 [2048, 2816], P(None, 'expert'), may hold values from -0.125 to 0.125
- s_up: bfloat16 [2048, 2816], P(None, 'expert'), may hold values from -0.125 to 0.125
- s_down: bfloat16 [2816, 2048], P('expert'), may hold values from -0.15625 to 0.15625
Outputs:
- mixed: bfloat16 [2048, 2048], P('dp', 'expert')
Inputs may be any that keep to these rules, and one draw needn't show every extreme that they name: `routes`: each row names 6 different experts. Within each aligned block of 256 rows (the rows of one index of dp) no expert is named by more than 32 rows; some expert is named by exactly 32 rows in some block of every draw.
All inputs are finite; a program needn't handle non-finite values.
Results may differ from a plain program's by a relative error of at most 0.013.
Values may be sent and summed in bfloat16 or wider, within the bound.
A program may use at most 128 MiB of HBM per device.

v0:
```python
import jax
import jax.numpy as jnp
from jax import lax
from jax.sharding import PartitionSpec as P

CAP = 32


def body(tokens, routes, gates, w_gate, w_up, w_down, s_gate, s_up, s_down):
    tok_rows, width = tokens.shape
    local_experts = w_gate.shape[0]
    groups = lax.axis_size("dp")
    members = lax.axis_size("expert")
    experts_all = local_experts * groups
    top_count = routes.shape[1]
    capacity = CAP
    quarter = width // members
    labels = jnp.arange(experts_all, dtype=jnp.int32)
    matches = (routes[:, :, None] == labels[None, None, :]).astype(jnp.int32)
    counts = jnp.sum(matches, axis=1)
    before = jnp.cumsum(counts, axis=0) - counts
    slots = jnp.sum(matches * before[:, None, :], axis=2)
    dest = routes * capacity + slots
    token_ids = jnp.repeat(jnp.arange(tok_rows, dtype=jnp.int32), top_count)
    sources = (
        jnp.full((experts_all * capacity,), tok_rows, jnp.int32).at[dest.reshape(-1)].set(token_ids)
    )
    padded = jnp.concatenate([tokens, jnp.zeros((1, width), tokens.dtype)], axis=0)
    outgoing = padded[sources].reshape(groups, local_experts, capacity, width)
    offset = lax.axis_index("expert") * quarter
    outgoing = lax.dynamic_slice_in_dim(outgoing, offset, quarter, 3)
    received = lax.all_to_all(outgoing, "dp", split_axis=0, concat_axis=0, tiled=True)
    received = lax.all_gather(received, "expert", axis=3, tiled=True)
    gate = jnp.einsum("sjcd,jdf->sjcf", received, w_gate, preferred_element_type=jnp.float32)
    up = jnp.einsum("sjcd,jdf->sjcf", received, w_up, preferred_element_type=jnp.float32)
    hidden = (jax.nn.silu(gate) * up).astype(jnp.bfloat16)
    partial_value = jnp.einsum("sjcf,jfd->sjcd", hidden, w_down, preferred_element_type=jnp.float32)
    summed = lax.psum_scatter(
        partial_value.astype(jnp.bfloat16), "expert", scatter_dimension=3, tiled=True
    )
    returned = lax.all_to_all(summed, "dp", split_axis=0, concat_axis=0, tiled=True)
    flat = returned.reshape(experts_all * capacity, quarter)
    picked = flat[dest].astype(jnp.float32)
    routed = jnp.einsum("tk,tkd->td", gates, picked)
    shared_gate = jnp.dot(tokens, s_gate, preferred_element_type=jnp.float32)
    shared_up = jnp.dot(tokens, s_up, preferred_element_type=jnp.float32)
    shared_hidden = (jax.nn.silu(shared_gate) * shared_up).astype(jnp.bfloat16)
    shared_part = jnp.dot(shared_hidden, s_down, preferred_element_type=jnp.float32)
    shared_out = lax.psum_scatter(
        shared_part.astype(jnp.bfloat16), "expert", scatter_dimension=1, tiled=True
    ).astype(jnp.float32)
    return (shared_out + routed).astype(jnp.bfloat16)


def solution(mesh):
    placed = (
        P("dp", None),
        P("dp", None),
        P("dp", None),
        P("dp", None, "expert"),
        P("dp", None, "expert"),
        P("dp", "expert", None),
        P(None, "expert"),
        P(None, "expert"),
        P("expert", None),
    )
    return jax.shard_map(
        body, mesh=mesh, in_specs=placed, out_specs=P("dp", "expert"), check_vma=False
    )
```

profile of v0, /device:TPU:0, one launch (start us, length us, event | category | flops | bytes accessed | tf_op | source)
XLA Modules:
  0.0 341.5 jit_solution(1969258154155409684)
XLA Ops:
  6.5 0.9 convert_reduce_fusion
  7.5 0.6 reduce-window.6
  8.4 0.8 select_reduce_fusion
  9.1 0.7 compare_select_fusion.1
  10.3 6.2 %scatter_custom_fusion = s32[2048]{0:T(1024)S(1)} fusion(s32[1536]{0:T(1024)S(1)} %fusion.19, s32[1536]{0:T(1024)S(1)} %reshape.78, s32[]{:T(128)} %constant.11.clone.1), kind=kCustom, calls=%fused_computation.38 | custom fusion | bytes 8196 | tf_op jit(solution)/shard_map/scatter | solution.py:26
  16.5 2.4 concatenate.3
  19.0 17.7 %gather_fusion = bf16[2048,2048]{1,0:T(8,128)(2,1)} fusion(bf16[257,2048]{1,0:T(8,128)(2,1)} %concatenate.3, s32[2048]{0:T(1024)S(1)} %fusion.18), kind=kCustom, calls=%fused_computation | custom fusion | bytes 16785408 | tf_op jit(solution)/shard_map/gather | solution.py:29
  36.7 1.8 constant_dynamic-slice_fusion
  38.5 55.3 %all_to_all.10 = bf16[8,8,32,512]{3,2,1,0:T(8,128)(2,1)S(1)} all-to-all(bf16[8,8,32,512]{3,2,1,0:T(8,128)(2,1)S(1)} %constant_dynamic-slice_fusion), channel_id=1, replica_groups=mesh['dp'=8,'expert'=4] {'dp'}, dimensions={0} | all-to-all | bytes 4194304 | tf_op jit(solution)/shard_map/all_to_all | solution.py:32
  93.8 1.6 copy.30
  95.7 57.2 %all-gather.2.cloned.1.call-done = bf16[8,8,32,2048]{3,2,0,1:T(8,128)(2,1)} async-done(((bf16[8,8,32,512]{3,2,0,1:T(8,128)(2,1)}), bf16[8,8,32,2048]{3,2,0,1:T(8,128)(2,1)}) %all-gather.2.cloned.1.call-update) | async-done | bytes 8388624 | tf_op jit(solution)/shard_map/all_gather | solution.py:33
  152.9 12.9 %fusion.4 = f32[8,8,32,352]{3,2,1,0:T(8,128)} fusion(bf16[8,8,32,2048]{3,2,0,1:T(8,128)(2,1)} %all-gather.2.cloned.1.call-done, bf16[8,2048,352]{1,2,0:T(8,128)(2,1)} %param.12), kind=kOutput, calls=%fused_computation.7 | convolution fusion | flops 2952790016 | bytes 22806528 | tf_op jit(solution)/shard_map/sjcd,jdf->sjcf/dot_general | solution.py:34
  165.9 13.3 %fusion.8 = bf16[8,8,32,352]{3,2,0,1:T(8,128)(2,1)} fusion(f32[8,8,32,352]{3,2,1,0:T(8,128)} %fusion.4, bf16[8,8,32,2048]{3,2,0,1:T(8,128)(2,1)} %all-gather.2.cloned.1.call-done, bf16[8,2048,352]{1,2,0:T(8,128)(2,1)} %param.13), kind=kOutput, calls=%fused_computation.11 | convolution fusion | flops 2957115392 | bytes 24248320 | tf_op jit(solution)/shard_map/sjcd,jdf->sjcf/dot_general | solution.py:35
  179.1 12.5 %convert_bitcast_fusion = bf16[8,8,32,2048]{3,2,0,1:T(8,128)(2,1)} fusion(bf16[8,8,32,352]{3,2,0,1:T(8,128)(2,1)} %fusion.8, bf16[8,352,2048]{2,1,0:T(8,128)(2,1)} %param.14), kind=kOutput, calls=%fused_computation.9 | convolution fusion | flops 2956984320 | bytes 21364736 | tf_op jit(solution)/shard_map/sjcf,jfd->sjcd/dot_general | solution.py:37
  191.7 71.4 %reduce-scatter.5.cloned.1.call-done = bf16[8,8,32,512]{3,2,0,1:T(8,128)(2,1)} async-done(((bf16[8,8,32,2048]{3,2,0,1:T(8,128)(2,1)}), bf16[8,8,32,512]{3,2,0,1:T(8,128)(2,1)}) %reduce-scatter.5.cloned.1.call-update) | async-done | bytes 2097168 | tf_op jit(solution)/shard_map/reduce_scatter | solution.py:38
  263.0 3.1 copy.31
  266.2 5.5 %all-to-all-start.1 = ((bf16[8,8,32,512]{3,2,1,0:T(8,128)(2,1)}), bf16[8,8,32,512]{3,2,1,0:T(8,128)(2,1)}, u32[]{:S(2)}, u32[]{:S(2)}) async-start(bf16[8,8,32,512]{3,2,1,0:T(8,128)(2,1)} %copy.31), calls=%async_computation.3 | async-start | bytes 4194304 | tf_op jit(solution)/shard_map/all_to_all | solution.py:41
  272.0 4.0 %fusion.23 = f32[256,704]{0,1:T(8,128)} fusion(bf16[256,2048]{1,0:T(8,128)(2,1)} %param.9, bf16[2048,704]{0,1:T(8,128)(2,1)} %param.15), kind=kOutput, calls=%fused_computation.42 | convolution fusion | flops 738197504 | bytes 4653056 | tf_op jit(solution)/shard_map/dot_general | solution.py:45
  275.9 6.6 %convolution_convert_fusion = bf16[256,2048]{1,0:T(8,128)(2,1)} fusion(bf16[704,2048]{1,0:T(8,128)(2,1)S(1)} %copy-done, bf16[256,2048]{1,0:T(8,128)(2,1)} %param.9, bf16[2048,704]{0,1:T(8,128)(2,1)} %param.16, f32[256,704]{0,1:T(8,128)} %fusion.23), kind=kOutput, calls=%fused_computation.17 | convolution fusion | flops 1478000640 | bytes 8585216 | tf_op jit(solution)/shard_map/dot_general | solution.py:48
  283.0 36.9 %all-to-all-done.1 = bf16[8,8,32,512]{3,2,1,0:T(8,128)(2,1)} async-done(((bf16[8,8,32,512]{3,2,1,0:T(8,128)(2,1)}), bf16[8,8,32,512]{3,2,1,0:T(8,128)(2,1)}, u32[]{:S(2)}, u32[]{:S(2)}) %all-to-all-start.1) | async-done | bytes 2097184 | tf_op jit(solution)/shard_map/all_to_all | solution.py:41
  319.9 7.4 %gather_fusion.1 = bf16[1536,512]{1,0:T(8,128)(2,1)} fusion(bf16[2048,512]{1,0:T(8,128)(2,1)} %bitcast.12, s32[2048]{0:T(1024)S(1)} %pad_clamp_fusion), kind=kCustom, calls=%fused_computation.1 | custom fusion | bytes 3151872 | tf_op jit(solution)/shard_map/gather | solution.py:43
  327.2 3.7 %reshape.67 = bf16[256,6,512]{2,1,0:T(8,128)(2,1)} reshape(bf16[1536,512]{1,0:T(8,128)(2,1)} %gather_fusion.1) | data formatting | bytes 3145728 | tf_op jit(solution)/shard_map/gather | solution.py:43
  331.0 2.3 fusion.24
  333.3 1.7 fusion.15
  (26 shorter events, 1.8 us)
Async XLA Ops:
  6.5 269.4 %copy-start = (bf16[704,2048]{1,0:T(8,128)(2,1)S(1)}, bf16[704,2048]{1,0:T(8,128)(2,1)}, u32[]{:S(2)}) copy-start(bf16[704,2048]{1,0:T(8,128)(2,1)} %param.17) | copy-start | bytes 8650756
  6.5 146.4 %all-gather.2.cloned.1.call-start = ((), (), s32[]{:S(2)}) async-start(), calls=%async_computation.5 | async-start | bytes 10485760 | tf_op jit(solution)/shard_map/all_gather | solution.py:33
  95.5 167.6 %reduce-scatter.5.cloned.1.call-start = ((), (), s32[]{:S(2)}) async-start(), calls=%async_computation.6 | async-start | bytes 10485760 | tf_op jit(solution)/shard_map/reduce_scatter | solution.py:38
  266.2 53.7 %all-to-all-start.1 = ((bf16[8,8,32,512]{3,2,1,0:T(8,128)(2,1)}), bf16[8,8,32,512]{3,2,1,0:T(8,128)(2,1)}, u32[]{:S(2)}, u32[]{:S(2)}) async-start(bf16[8,8,32,512]{3,2,1,0:T(8,128)(2,1)} %copy.31), calls=%async_computation.3 | async-start | bytes 4194304 | tf_op jit(solution)/shard_map/all_to_all | solution.py:41
  271.7 61.6 %reduce-scatter.3.cloned.1.call-start = ((), (), s32[]{:S(2)}) async-start(), calls=%async_computation.4 | async-start | bytes 1310720 | tf_op jit(solution)/shard_map/reduce_scatter | solution.py:49
  275.9 6.9 %copy-start.1 = (f32[256,6]{0,1:T(8,128)S(1)}, f32[256,6]{0,1:T(8,128)}, u32[]{:S(2)}) copy-start(f32[256,6]{0,1:T(8,128)} %param.11) | copy-start | bytes 18436
Sparse Core Ops, SparseCore 0:
  95.6 57.2 all-gather.1
  191.8 71.2 reduce-scatter.4
  282.7 25.0 reduce-scatter.2
where the time goes:
time: 342 us
  waiting for transfers between devices  166 us (49%)
  blocking collectives  55.3 us (16%)
  matrix products  51.5 us (15%)
  local copies, waits for them, and re-layouts  45.1 us (13%)
  between operations  13.3 us (4%)
  starting transfers between devices  5.99 us (2%)
  other arithmetic  4.86 us (1%)
    reduce_scatter x1, waiting for transfers between devices, body(): lax.psum_scatter(partial_value.astype(jnp.bfloat16), 'expert', scatter_di...  71.4 us
    all_gather x1, waiting for transfers between devices, body(): received = lax.all_gather(received, 'expert', axis=3, tiled=True)  57.2 us
    all_to_all x1, blocking collectives, body(): lax.all_to_all(outgoing, 'dp', split_axis=0, concat_axis=0, tiled=True)  55.3 us
    all_to_all x1, waiting for transfers between devices, body(): lax.all_to_all(summed, 'dp', split_axis=0, concat_axis=0, tiled=True)  36.9 us
    gather x1, local copies, waits for them, and re-layouts, body(): outgoing = padded[sources].reshape(groups, local_experts, capacity, width)  17.7 us
    dot_general x1, matrix products, body(): jnp.einsum('sjcd,jdf->sjcf', received, w_up, preferred_element_type=jnp.f...  13.3 us
    dot_general x1, matrix products, body(): jnp.einsum('sjcd,jdf->sjcf', received, w_gate, preferred_element_type=jnp...  12.9 us
    dot_general x1, matrix products, body(): jnp.einsum('sjcf,jfd->sjcd', hidden, w_down, preferred_element_type=jnp.f...  12.5 us
  transfers between devices with their start and end apart: 4, of which 3 were waited for; matrix products, arithmetic and copies ran while one was open for 7% of the time, Pallas kernels for 0%

commit v1 on v0

v1 whole, which is shorter than its diff:
```python
import jax
import jax.numpy as jnp
from jax import lax
from jax.experimental import pallas as pl
from jax.experimental.pallas import tpu as pltpu
from jax.sharding import PartitionSpec as P

CAP = 32
EXTRA = 128
AXES = ("dp", "expert")


def experts_kernel(x_ref, g_ref, wg_ref, wu_ref, wd_ref, out_ref):
    groups, cap, width = x_ref.shape
    members, _, _, part = out_ref.shape
    x = x_ref[...].reshape(groups * cap, width)
    gate = jnp.dot(x, wg_ref[0], preferred_element_type=jnp.float32)
    up = jnp.dot(x, wu_ref[0], preferred_element_type=jnp.float32)
    scale = g_ref[0]
    hidden = (gate / (1.0 + jnp.exp(-gate)) * up * scale).astype(jnp.bfloat16)
    for f in range(members):
        value = jnp.dot(
            hidden, wd_ref[0, :, f * part:(f + 1) * part], preferred_element_type=jnp.float32
        )
        out_ref[f] = value.astype(jnp.bfloat16).reshape(groups, cap, part)


def run_experts(x, slot_gates, w_gate, w_up, w_down, members):
    groups, slots, width = x.shape
    local, _, units = w_gate.shape
    cap = slots // local
    rows = groups * cap
    part = width // members
    return pl.pallas_call(
        experts_kernel,
        grid=(local,),
        out_shape=jax.ShapeDtypeStruct((members, groups, slots, part), jnp.bfloat16),
        in_specs=[
            pl.BlockSpec((groups, cap, width), lambda e: (0, e, 0)),
            pl.BlockSpec((1, rows, 1), lambda e: (e, 0, 0)),
            pl.BlockSpec((1, width, units), lambda e: (e, 0, 0)),
            pl.BlockSpec((1, width, units), lambda e: (e, 0, 0)),
            pl.BlockSpec((1, units, width), lambda e: (e, 0, 0)),
        ],
        out_specs=pl.BlockSpec((members, groups, cap, part), lambda e: (0, 0, e, 0)),
        compiler_params=pltpu.CompilerParams(
            dimension_semantics=("arbitrary",), vmem_limit_bytes=60 << 20
        ),
        cost_estimate=pl.CostEstimate(
            flops=6 * rows * local * width * units,
            bytes_accessed=6 * local * width * units + 4 * rows * local * width,
            transcendentals=rows * local * units,
        ),
    )(x, slot_gates, w_gate, w_up, w_down)


def body(tokens, routes, gates, w_gate, w_up, w_down, s_gate, s_up, s_down):
    tok_rows, width = tokens.shape
    local = w_gate.shape[0]
    groups = lax.axis_size("dp")
    members = lax.axis_size("expert")
    top = routes.shape[1]
    part = width // members
    mine = tok_rows // members
    group = lax.axis_index("dp")
    member = lax.axis_index("expert")

    high = lax.reduce_precision(gates, 8, 7)
    middle = lax.reduce_precision(gates - high, 8, 7)
    low = gates - high - middle
    extra = jnp.concatenate([routes.astype(jnp.float32), high, middle, low], axis=1)
    extra = jnp.pad(extra.astype(jnp.bfloat16), ((0, 0), (0, EXTRA - extra.shape[1])))
    block = jnp.concatenate([tokens, extra], axis=1)
    block = lax.dynamic_slice_in_dim(block, member * mine, mine, 0)
    gathered = lax.all_gather(block, AXES, axis=0, tiled=True)

    shared_gate = jnp.dot(tokens, s_gate, preferred_element_type=jnp.float32)
    shared_up = jnp.dot(tokens, s_up, preferred_element_type=jnp.float32)
    shared_hidden = (jax.nn.silu(shared_gate) * shared_up).astype(jnp.bfloat16)
    shared_part = jnp.dot(shared_hidden, s_down, preferred_element_type=jnp.float32)

    gathered = gathered.reshape(groups, tok_rows, width + EXTRA)
    table = gathered[:, :, width:width + 4 * top].astype(jnp.float32)
    names = table[:, :, :top]
    values = table[:, :, top:2 * top] + table[:, :, 2 * top:3 * top] + table[:, :, 3 * top:]
    own = (group * local + jnp.arange(local)).astype(jnp.float32)
    hits = names[:, :, :, None] == own
    match = jnp.any(hits, axis=2)
    weight = jnp.sum(jnp.where(hits, values[:, :, :, None], 0.0), axis=2)
    earlier = jnp.tri(tok_rows, tok_rows, -1, dtype=jnp.bfloat16)
    before = jnp.einsum(
        "tu,suj->sjt", earlier, match.astype(jnp.bfloat16), preferred_element_type=jnp.float32
    )
    before = jnp.where(jnp.swapaxes(match, 1, 2), before, -1.0)
    slot = jnp.arange(CAP).astype(jnp.float32)
    chosen = before[:, :, None, :] == slot[:, None]
    slot_gates = jnp.sum(
        jnp.where(chosen, jnp.swapaxes(weight, 1, 2)[:, :, None, :], 0.0), axis=3
    )
    slot_gates = jnp.swapaxes(slot_gates, 0, 1).reshape(local, groups * CAP, 1)
    pick = chosen.astype(jnp.bfloat16).reshape(groups, local * CAP, tok_rows)

    x = jnp.einsum(
        "sqt,std->sqd", pick, gathered[:, :, :width], preferred_element_type=jnp.float32
    ).astype(jnp.bfloat16)
    outs = run_experts(x, slot_gates, w_gate, w_up, w_down, members)
    total = jnp.einsum("sqt,fsqd->sftd", pick, outs, preferred_element_type=jnp.float32)
    here = (jnp.arange(groups) == group)[:, None, None, None]
    shared = jnp.swapaxes(shared_part.reshape(tok_rows, members, part), 0, 1)
    total = (total + jnp.where(here, shared[None], 0.0)).astype(jnp.bfloat16)
    total = total.reshape(groups * members, tok_rows, part)
    return lax.psum_scatter(total, AXES, scatter_dimension=0, tiled=False)


def solution(mesh):
    placed = (
        P("dp", None),
        P("dp", None),
        P("dp", None),
        P("dp", None, "expert"),
        P("dp", None, "expert"),
        P("dp", "expert", None),
        P(None, "expert"),
        P(None, "expert"),
        P("expert", None),
    )
    return jax.shard_map(
        body, mesh=mesh, in_specs=placed, out_specs=P("dp", "expert"), check_vma=False
    )
```

time: 342 us -> 311 us (0.909)
  blocking collectives: 55.3 us -> 0 us
  Pallas kernels: 0 us -> 23.5 us
  waiting for transfers between devices: 166 us -> 189 us
  matrix products: 51.5 us -> 29.4 us
  starting transfers between devices: 5.99 us -> 0.04 us
    reduce_scatter x2 -> x1, waiting for transfers between devices: 71.4 us -> 149 us  [body(): return lax.psum_scatter(total, AXES, scatter_dimension=0, tiled=False)]
    all_to_all x1 -> x0, blocking collectives: 55.3 us -> none  [body(): lax.all_to_all(outgoing, 'dp', split_axis=0, concat_axis=0, tiled=True)]
    all_to_all x1 -> x0, waiting for transfers between devices: 36.9 us -> none  [body(): lax.all_to_all(summed, 'dp', split_axis=0, concat_axis=0, tiled=True)]
    unnamed x5 -> x9, local copies, waits for them, and re-layouts: 0.18 us -> 31.8 us
    dot_general x5 -> x3, matrix products: 47.5 us -> 18.5 us  [the longest x1 9.31 us: body(): jnp.einsum('sqt,fsqd->sftd', pick, outs, preferred_element_type=jnp.float32)]
    gather x3 -> x0, local copies, waits for them, and re-layouts: 28.8 us -> none  [the longest x1 17.7 us: body(): outgoing = padded[sources].reshape(groups, local_experts, capacity, width)]
    pallas_call x0 -> x1, Pallas kernels: none -> 23.5 us  [run_experts(): pl.pallas_call(experts_kernel, grid=(local,), out_shape=jax.ShapeDtypeStr...]
    all_gather x1, waiting for transfers between devices: 57.2 us -> 39.4 us  [body(): gathered = lax.all_gather(block, AXES, axis=0, tiled=True)]
  transfers between devices with their start and end apart: 4 -> 2, of which waited for: 3 -> 2; matrix products, arithmetic and copies ran while one was open for 7% -> 14% of each run, Pallas kernels for 0% -> 0%
where the time goes in v1:
time: 311 us; the launch traced here: 310 us
  waiting for transfers between devices  189 us (61%)
  local copies, waits for them, and re-layouts  47.8 us (15%)
  matrix products  29.4 us (9%)
  Pallas kernels  23.5 us (8%)
  between operations  13.5 us (4%)
  other arithmetic  7.3 us (2%)
    reduce_scatter x1, waiting for transfers between devices, body(): return lax.psum_scatter(total, AXES, scatter_dimension=0, tiled=False)  149 us
    all_gather x1, waiting for transfers between devices, body(): gathered = lax.all_gather(block, AXES, axis=0, tiled=True)  39.4 us
    unnamed x9, local copies, waits for them, and re-layouts  31.8 us
    pallas_call x1, Pallas kernels, run_experts(): pl.pallas_call(experts_kernel, grid=(local,), out_shape=jax.ShapeDtypeStr...  23.5 us
    reshape x1, local copies, waits for them, and re-layouts, body(): total = total.reshape(groups * members, tok_rows, part)  12 us
    dot_general x1, matrix products, body(): jnp.einsum('sqt,fsqd->sftd', pick, outs, preferred_element_type=jnp.float32)  9.31 us
    dot_general x1, matrix products, body(): jnp.einsum('sqt,std->sqd', pick, gathered[:, :, :width], preferred_elemen...  8.97 us
    reshape x1, matrix products, body(): shared = jnp.swapaxes(shared_part.reshape(tok_rows, members, part), 0, 1)  6.91 us
  transfers between devices with their start and end apart: 2, of which 2 were waited for; matrix products, arithmetic and copies ran while one was open for 14% of the time, Pallas kernels for 0%

profile of v1, /device:TPU:0, one launch (start us, length us, event | category | flops | bytes accessed | tf_op | source)
XLA Modules:
  0.0 310.2 jit_solution(3846101421583929412)
XLA Ops:
  6.5 0.9 reduce-precision_convert_fusion.1
  7.4 0.7 convert_convert_fusion
  8.1 0.1 copy.45
  8.3 1.7 fusion.18
  10.1 16.2 %copy.36.wg_ref = bf16[8,2048,352]{2,1,0:T(8,128)(2,1)} copy(bf16[8,2048,352]{1,2,0:T(8,128)(2,1)} %param.12) | data formatting | bytes 23068672 | tf_op args[3]
  26.4 15.4 %copy.37.wu_ref = bf16[8,2048,352]{2,1,0:T(8,128)(2,1)} copy(bf16[8,2048,352]{1,2,0:T(8,128)(2,1)} %param.13) | data formatting | bytes 23068672 | tf_op args[4]
  41.8 4.0 %fusion.24 = f32[256,704]{0,1:T(8,128)} fusion(bf16[256,2048]{1,0:T(8,128)(2,1)} %param.9, bf16[2048,704]{0,1:T(8,128)(2,1)} %param.15), kind=kOutput, calls=%fused_computation.45 | convolution fusion | flops 738197504 | bytes 4653056 | tf_op jit(solution)/shard_map/dot_general | solution.py:77
  45.8 6.9 %fusion.9 = f32[256,2048]{0,1:T(8,128)} fusion(bf16[704,2048]{1,0:T(8,128)(2,1)S(1)} %copy-done, bf16[256,2048]{1,0:T(8,128)(2,1)} %param.9, bf16[2048,704]{0,1:T(8,128)(2,1)} %param.16, f32[256,704]{0,1:T(8,128)} %fusion.24), kind=kOutput, calls=%fused_computation.16 | convolution fusion | flops 1477476352 | bytes 9633792 | tf_op jit(solution)/shard_map/reshape | solution.py:109
  52.7 39.4 %all-gather.2.cloned.1.call-done = bf16[2048,2176]{1,0:T(8,128)(2,1)} async-done(((bf16[64,2176]{1,0:T(8,128)(2,1)}), bf16[2048,2176]{1,0:T(8,128)(2,1)}) %all-gather.2.cloned.1.call-update) | async-done | bytes 8912912 | tf_op jit(solution)/shard_map/all_gather | solution.py:75
  92.1 1.1 slice_convert_fusion
  93.2 1.8 slice_add_fusion
  95.1 1.5 copy.32
  96.6 0.3 copy.33
  97.0 0.1 compare_reduce_fusion
  97.1 0.1 fusion.16
  97.2 0.2 convolution_select_fusion
  97.4 0.4 select_reduce_fusion
  97.9 2.0 reshape.39.g_ref
  99.9 0.4 bitcast_compare_fusion
  100.3 9.0 %fusion.4.x_ref = bf16[8,256,2048]{2,1,0:T(8,128)(2,1)} fusion(pred[8,256,256]{2,1,0:T(32,128)(4,1)S(1)} %bitcast_compare_fusion, bf16[8,256,2176]{2,1,0:T(8,128)(2,1)} %bitcast.32), kind=kOutput, calls=%fused_computation.5 | convolution fusion | flops 2151677952 | bytes 17301504 | tf_op jit(solution)/shard_map/sqt,std->sqd/dot_general | solution.py:103
  109.3 23.5 %shard_map.91 = bf16[4,8,256,512]{3,2,1,0:T(8,128)(2,1)} custom-call(bf16[8,256,2048]{2,1,0:T(8,128)(2,1)} %fusion.4.x_ref, f32[8,256,1]{2,1,0:T(8,128)} %reshape.39.g_ref, bf16[8,2048,352]{2,1,0:T(8,128)(2,1)} %copy.36.wg_ref, bf16[8,2048,352]{2,1,0:T(8,128)(2,1)} %copy.37.wu_ref, bf16[8,352,2048]{2,1,0:T(8,128)(2,1)} %wd_ref.1), custom_call_target="tpu_custom_call" | custom-call | flops 8858370048 | bytes 51380224 | tf_op jit(solution)/shard_map/pallas_call | solution.py:34
  132.8 9.3 %fusion = bf16[8,4,256,512]{2,3,1,0:T(8,128)(2,1)} fusion(bf16[4,8,256,512]{3,2,1,0:T(8,128)(2,1)} %shard_map.91, f32[4,256,512]{1,2,0:T(8,128)S(1)} %bitcast.36, pred[8]{0:T(512)(128)(4,1)S(1)} %iota_compare_fusion.2, pred[8,256,256]{2,1,0:T(32,128)(4,1)S(1)} %bitcast_compare_fusion), kind=kOutput, calls=%fused_computation.1 | convolution fusion | flops 2160066560 | bytes 19398664 | tf_op jit(solution)/shard_map/sqt,fsqd->sftd/dot_general | solution.py:107
  142.1 12.0 %copy.40 = bf16[32,256,512]{2,1,0:T(8,128)(2,1)} copy(bf16[32,256,512]{1,2,0:T(8,128)(2,1)} %bitcast.33) | data formatting | bytes 16777216 | tf_op jit(solution)/shard_map/reshape | solution.py:111
  154.2 149.2 %reduce-scatter.2.cloned.1.call-done = bf16[1,256,512]{2,1,0:T(8,128)(2,1)} async-done(((bf16[32,256,512]{2,1,0:T(8,128)(2,1)}), bf16[1,256,512]{2,1,0:T(8,128)(2,1)}) %reduce-scatter.2.cloned.1.call-update) | async-done | bytes 262160 | tf_op jit(solution)/shard_map/reduce_scatter | solution.py:112
  (18 shorter events, 0.2 us)
Async XLA Ops:
  6.5 39.2 %copy-start = (bf16[704,2048]{1,0:T(8,128)(2,1)S(1)}, bf16[704,2048]{1,0:T(8,128)(2,1)}, u32[]{:S(2)}) copy-start(bf16[704,2048]{1,0:T(8,128)(2,1)} %param.17) | copy-start | bytes 8650756
  6.5 85.6 %all-gather.2.cloned.1.call-start = ((), (), s32[]{:S(2)}) async-start(), calls=%async_computation.1 | async-start | bytes 9191424 | tf_op jit(solution)/shard_map/all_gather | solution.py:75
  10.0 293.4 %reduce-scatter.2.cloned.1.call-start = ((), (), s32[]{:S(2)}) async-start(), calls=%async_computation.2 | async-start | bytes 8650752 | tf_op jit(solution)/shard_map/reduce_scatter | solution.py:112
  109.3 23.5 %copy-start.2 = (f32[256,2048]{0,1:T(8,128)S(1)}, f32[256,2048]{0,1:T(8,128)}, u32[]{:S(2)}) copy-start(f32[256,2048]{0,1:T(8,128)} %fusion.9) | copy-start | bytes 6291460
  142.1 161.2 %copy-start.1 = (bf16[704,2048]{1,0:T(8,128)(2,1)S(1)}, bf16[704,2048]{1,0:T(8,128)(2,1)}, u32[]{:S(2)}) copy-start(bf16[704,2048]{1,0:T(8,128)(2,1)} %param.17) | copy-start | bytes 8650756
Sparse Core Ops, SparseCore 0:
  10.2 81.8 all-gather.1
  154.3 148.9 reduce-scatter.1
